TPU v7x, 32 devices: a whole 2x2x4 slice. The times are simulated.
32 devices in a mesh: gx: 4 (over z), gy: 8 (over y, x, core).
Axes of the slice: x: 2, y: 2, z: 4, core: 2. Of those that a mesh axis runs over, the one named last changes fastest.
Arguments:
- tables: float32 [2, 262144, 128], P(None, ('gx', 'gy')), may hold values from -0.9 to 0.9
- cold_rows: int32 [32, 2, 32, 16], P(('gx', 'gy')), may hold values from 0 to 8191, as said below
- cold_bags: int32 [32, 2, 32, 16], P(('gx', 'gy')), may hold values from -1 to 127, as said below
- hot_rows: int32 [2, 256], replicated, may hold values from 0 to 262143
- hot_ids: int32 [4096, 2, 8], P(('gx', 'gy')), may hold values from 0 to 255
Outputs:
- pooled: float32 [4096, 2, 128], P(('gx', 'gy'))
Inputs may be any that keep to these rules, and one draw needn't show every extreme that they name: `cold_rows`: every entry names one of the owner's 8192 rows. `cold_bags`: live slots of one sender, table and owner come first, the empty ones (-1) after them; in every draw each table has an owner whose 16 slots are all live from every sender.
All inputs are finite; a program needn't handle non-finite values.
Results may differ from a plain program's by a relative error of at most 0.0003.
Values sent between devices are 32-bit elements; how exact they have to be, the bound alone decides.
A program may use at most 64 MiB of HBM per device.

v0:
```python
import math

import jax
import jax.numpy as jnp
from jax import lax
from jax.sharding import PartitionSpec as P


def pick_rows(table, indices):
    count = indices.shape[0]
    block = math.gcd(512, count)
    row_ids = jnp.arange(table.shape[0], dtype=jnp.int32)
    grouped = indices.reshape(count // block, block)

    def one_block(wanted):
        selector = (wanted[:, None] == row_ids[None, :]).astype(jnp.float32)
        return jnp.dot(
            selector, table, precision=lax.Precision.HIGHEST, preferred_element_type=jnp.float32
        )

    return lax.map(one_block, grouped).reshape(count, table.shape[1])


def body(tables, cold_rows, cold_bags, hot_rows, hot_ids):
    axis_x = lax.axis_size("gx")
    axis_y = lax.axis_size("gy")
    peer_count = axis_x * axis_y
    table_count, rows_dev, emb_width = tables.shape
    slot_cap = cold_rows.shape[3]
    batch_rows = hot_ids.shape[0]
    hot_count = hot_rows.shape[1]
    my_index = lax.axis_index(("gx", "gy"))
    hot_owner = hot_rows // rows_dev
    local_rows = jnp.where(hot_owner == my_index, hot_rows - my_index * rows_dev, -1)
    picked = jax.vmap(pick_rows)(tables, local_rows)
    hot_table = lax.psum(picked, ("gx", "gy"))
    matches = jnp.sum(
        (
            hot_ids[:, :, :, None] == jnp.arange(hot_count, dtype=jnp.int32)[None, None, None, :]
        ).astype(jnp.float32),
        axis=2,
    )
    hot_part = jnp.einsum("bth,thd->btd", matches, hot_table, precision=lax.Precision.HIGHEST)
    my_rows = cold_rows[0]
    my_bags = cold_bags[0]
    got_rows, got_bags = (
        lax.all_to_all(my_rows, ("gx", "gy"), split_axis=1, concat_axis=1, tiled=True),
        lax.all_to_all(my_bags, ("gx", "gy"), split_axis=1, concat_axis=1, tiled=True),
    )
    wanted_rows = jnp.where(got_bags >= 0, got_rows, -1)
    looked = jax.vmap(pick_rows)(tables, wanted_rows.reshape(table_count, -1))
    looked = looked.reshape(table_count, peer_count, slot_cap, emb_width)
    samples = jnp.arange(batch_rows, dtype=jnp.int32)
    returned = lax.all_to_all(looked, ("gx", "gy"), split_axis=1, concat_axis=1, tiled=True)
    onehot = (my_bags[:, None, :, :] == samples[None, :, None, None]).astype(jnp.float32)
    cold_part = jnp.einsum("tbpc,tpcd->btd", onehot, returned, precision=lax.Precision.HIGHEST)
    return cold_part + hot_part


def solution(mesh):
    return jax.shard_map(
        body,
        mesh=mesh,
        in_specs=(
            P(None, ("gx", "gy"), None),
            P(("gx", "gy"), None, None, None),
            P(("gx", "gy"), None, None, None),
            P(),
            P(("gx", "gy"), None, None),
        ),
        out_specs=P(("gx", "gy"), None, None),
        check_vma=False,
    )
```

profile of v0, /device:TPU:0, one launch (start us, length us, event | category | flops | bytes accessed | tf_op | source)
XLA Modules:
  0.0 203.2 jit_solution(9199264976657592994)
XLA Ops:
  6.5 1.4 copy.23
  7.9 7.3 %all-to-all-start.1 = ((s32[2,32,16]{2,0,1:T(2,128)}), s32[2,32,16]{2,0,1:T(2,128)S(1)}, u32[]{:S(2)}, u32[]{:S(2)}) async-start(s32[2,32,16]{2,0,1:T(2,128)} %bitcast.1), calls=%async_computation.1 | async-start | bytes 65536 | tf_op jit(solution)/shard_map/all_to_all | solution.py:47
  15.3 1.4 copy.22
  16.7 5.9 %all-to-all-done.1 = s32[2,32,16]{2,0,1:T(2,128)S(1)} async-done(((s32[2,32,16]{2,0,1:T(2,128)}), s32[2,32,16]{2,0,1:T(2,128)S(1)}, u32[]{:S(2)}, u32[]{:S(2)}) %all-to-all-start.1) | async-done | bytes 4128 | tf_op jit(solution)/shard_map/all_to_all | solution.py:47
  22.5 2.6 %all-to-all-start = ((s32[2,32,16]{2,0,1:T(2,128)}), s32[2,32,16]{2,0,1:T(2,128)S(1)}, u32[]{:S(2)}, u32[]{:S(2)}) async-start(s32[2,32,16]{2,0,1:T(2,128)} %bitcast), calls=%async_computation | async-start | bytes 65536 | tf_op jit(solution)/shard_map/all_to_all | solution.py:48
  25.1 7.2 %all-to-all-done = s32[2,32,16]{2,0,1:T(2,128)S(1)} async-done(((s32[2,32,16]{2,0,1:T(2,128)}), s32[2,32,16]{2,0,1:T(2,128)S(1)}, u32[]{:S(2)}, u32[]{:S(2)}) %all-to-all-start) | async-done | bytes 4128 | tf_op jit(solution)/shard_map/all_to_all | solution.py:48
  32.4 0.1 eq.74
  32.5 0.0 copy-start.1
  32.5 18.0 %fusion = f32[2,512,128]{2,1,0:T(8,128)S(1)} fusion(f32[2,8192,128]{2,1,0:T(8,128)} %param.5, s32[2,512]{1,0:T(2,128)S(1)} %eq.74), kind=kOutput, calls=%fused_computation.1 | convolution fusion | flops 12893290496 | bytes 8916992 | tf_op jit(solution)/shard_map/vmap()/while/body/eval_jaxpr/dot_general | solution.py:17
  50.5 0.0 copy-start
  50.5 0.9 copy.25
  51.4 2.6 %all-to-all-start.2 = ((f32[2,32,16,128]{3,2,0,1:T(8,128)}), f32[2,32,16,128]{3,2,0,1:T(8,128)S(1)}, u32[]{:S(2)}, u32[]{:S(2)}) async-start(f32[2,32,16,128]{3,2,0,1:T(8,128)} %copy.25), calls=%async_computation.2 | async-start | bytes 1048576 | tf_op jit(solution)/shard_map/all_to_all | solution.py:54
  54.0 0.2 all-reduce.2.cloned.1.call-start
  54.2 0.0 copy-done.1
  54.3 11.7 %fusion.2 = f32[2,256,128]{2,1,0:T(8,128)} fusion(f32[2,8192,128]{2,1,0:T(8,128)} %param.5, s32[2,256]{1,0:T(2,128)S(1)} %compare_select_fusion.1), kind=kOutput, calls=%fused_computation.4 | convolution fusion | flops 6446645248 | bytes 8652800 | tf_op jit(solution)/shard_map/vmap()/while/body/eval_jaxpr/dot_general | solution.py:17
  66.0 0.0 all-reduce.2.cloned.1.call-update
  66.0 0.0 copy-done
  66.0 0.1 copy.26
  66.2 0.8 convert_reduce_fusion
  67.0 2.6 %all-to-all-done.2 = f32[2,32,16,128]{3,2,0,1:T(8,128)S(1)} async-done(((f32[2,32,16,128]{3,2,0,1:T(8,128)}), f32[2,32,16,128]{3,2,0,1:T(8,128)S(1)}, u32[]{:S(2)}, u32[]{:S(2)}) %all-to-all-start.2) | async-done | bytes 524320 | tf_op jit(solution)/shard_map/all_to_all | solution.py:54
  69.6 1.5 convolution_bitcast_fusion
  71.1 122.8 %all-reduce.2.cloned.1.call-done = f32[2,256,128]{2,1,0:T(8,128)} async-done(((f32[2,256,128]{2,1,0:T(8,128)}), f32[2,256,128]{2,1,0:T(8,128)}) %all-reduce.2.cloned.1.call-update) | async-done | bytes 262160 | tf_op jit(solution)/shard_map/psum | solution.py:36
  194.0 1.6 fusion.4
  195.6 0.8 copy.29
  (3 shorter events, 0.0 us)
Async XLA Ops:
  7.9 14.6 %all-to-all-start.1 = ((s32[2,32,16]{2,0,1:T(2,128)}), s32[2,32,16]{2,0,1:T(2,128)S(1)}, u32[]{:S(2)}, u32[]{:S(2)}) async-start(s32[2,32,16]{2,0,1:T(2,128)} %bitcast.1), calls=%async_computation.1 | async-start | bytes 65536 | tf_op jit(solution)/shard_map/all_to_all | solution.py:47
  22.5 9.8 %all-to-all-start = ((s32[2,32,16]{2,0,1:T(2,128)}), s32[2,32,16]{2,0,1:T(2,128)S(1)}, u32[]{:S(2)}, u32[]{:S(2)}) async-start(s32[2,32,16]{2,0,1:T(2,128)} %bitcast), calls=%async_computation | async-start | bytes 65536 | tf_op jit(solution)/shard_map/all_to_all | solution.py:48
  32.5 21.8 %copy-start.1 = (s32[2,256]{1,0:T(2,128)S(1)}, s32[2,256]{1,0:T(2,128)}, u32[]{:S(2)}) copy-start(s32[2,256]{1,0:T(2,128)} %param.8) | copy-start | bytes 6148
  50.5 15.5 %copy-start = (s32[128,2,8]{0,2,1:T(8,128)S(1)}, s32[128,2,8]{0,2,1:T(8,128)}, u32[]{:S(2)}) copy-start(s32[128,2,8]{0,2,1:T(8,128)} %param.9) | copy-start | bytes 24580
  51.4 18.2 %all-to-all-start.2 = ((f32[2,32,16,128]{3,2,0,1:T(8,128)}), f32[2,32,16,128]{3,2,0,1:T(8,128)S(1)}, u32[]{:S(2)}, u32[]{:S(2)}) async-start(f32[2,32,16,128]{3,2,0,1:T(8,128)} %copy.25), calls=%async_computation.2 | async-start | bytes 1048576 | tf_op jit(solution)/shard_map/all_to_all | solution.py:54
  54.0 140.0 %all-reduce.2.cloned.1.call-start = ((), (), s32[]{:S(2)}) async-start(), calls=%async_computation.3 | async-start | bytes 524288 | tf_op jit(solution)/shard_map/psum | solution.py:36
Sparse Core Ops, SparseCore 0:
  66.1 127.7 all-reduce.1
where the time goes:
time: 204 us; the launch traced here: 203 us
  waiting for transfers between devices  139 us (68%)
  matrix products  32.8 us (16%)
  between operations  13.5 us (7%)
  starting transfers between devices  12.7 us (6%)
  local copies, waits for them, and re-layouts  4.66 us (2%)
    psum x1, waiting for transfers between devices, body(): hot_table = lax.psum(picked, ('gx', 'gy'))  123 us
    dot_general x2, matrix products, one_block(): jnp.dot(selector, table, precision=lax.Precision.HIGHEST, preferred_eleme...  29.7 us
    all_to_all x1, starting transfers between devices, body(): lax.all_to_all(my_rows, ('gx', 'gy'), split_axis=1, concat_axis=1, tiled=...  7.33 us
    all_to_all x1, waiting for transfers between devices, body(): lax.all_to_all(my_bags, ('gx', 'gy'), split_axis=1, concat_axis=1, tiled=...  7.25 us
    all_to_all x1, waiting for transfers between devices, body(): lax.all_to_all(my_rows, ('gx', 'gy'), split_axis=1, concat_axis=1, tiled=...  5.86 us
  transfers between devices with their start and end apart: 4, of which 4 were waited for; matrix products, arithmetic and copies ran while one was open for 8% of the time, Pallas kernels for 0%

commit v1 on v0

v1 whole, which is shorter than its diff:
```python
import functools

import jax
import jax.numpy as jnp
from jax import lax
from jax.experimental import pallas as pl
from jax.experimental.pallas import tpu as pltpu
from jax.sharding import PartitionSpec as P

MESH = pl.DeviceIdType.MESH
CHUNKS = 4


def split2(x):
    hi = x.astype(jnp.bfloat16)
    return hi, (x - hi.astype(jnp.float32)).astype(jnp.bfloat16)


def pool(weights, values):
    hi, lo = split2(values)
    return jnp.dot(weights, hi, preferred_element_type=jnp.float32) + jnp.dot(
        weights, lo, preferred_element_type=jnp.float32
    )


def kernel(nx, ny, tables_ref, rows_ref, bags_ref, hot_rows_ref, hot_ids_ref, out_ref,
           tab, idx_out, idx_in, idx_s, stage, recv, hot_stage, hot_in, hot_tab, onehot, counts,
           tab_sem, idx_send, idx_recv, idx_local, cold_send, cold_recv,
           hot_send, hot_recv, gat_send, gat_recv):
    peers = nx * ny
    tcount, rows_dev, width = tab.shape
    cap = rows_ref.shape[3]
    hot = hot_rows_ref.shape[1]
    share = hot_tab.shape[0] // peers
    batch = out_ref.shape[0]
    gx, gy = lax.axis_index("gx"), lax.axis_index("gy")
    me = gx * ny + gy

    def peer(i):
        px = lax.rem(gx + lax.rem(i, nx) + nx // 2, nx)
        py = lax.rem(gy + i // nx, ny)
        return px, py, px * ny + py

    self_at = (nx - nx // 2) % nx

    def others(fn):
        def step(i, carry):
            @pl.when(i != self_at)
            def _():
                fn(*peer(i))
            return carry
        lax.fori_loop(0, peers, step, 0)

    piece = rows_dev // CHUNKS
    loads = []
    for t in range(tcount):
        for c in range(CHUNKS):
            part = pl.ds(c * piece, piece)
            load = pltpu.make_async_copy(tables_ref.at[t, part], tab.at[t, part], tab_sem.at[t, c])
            load.start()
            loads.append(load)

    barrier = pltpu.get_barrier_semaphore()
    others(lambda px, py, p: pl.semaphore_signal(
        barrier, inc=1, device_id=(px, py), device_id_type=MESH))

    for p in range(peers):
        for t in range(tcount):
            idx_out[p, :, t * cap:(t + 1) * cap] = rows_ref[0, t, p:p + 1, :]
    idx_in[me] = idx_out[me]
    pl.semaphore_wait(barrier, peers - 1)

    def send_idx(px, py, p):
        pltpu.make_async_remote_copy(
            src_ref=idx_out.at[p], dst_ref=idx_in.at[me], send_sem=idx_send, recv_sem=idx_recv,
            device_id=(px, py), device_id_type=MESH).start()
    others(send_idx)

    for load in loads:
        load.wait()

    base = me * rows_dev

    def pick_hot(p):
        start = p * share
        t = start // hot
        first = start - t * hot
        for j in range(share):
            local = hot_rows_ref[t, first + j] - base
            mine = jnp.logical_and(local >= 0, local < rows_dev).astype(jnp.float32)
            at = jnp.clip(local, 0, rows_dev - 1)
            hot_stage[p, j:j + 1, :] = tab[t, pl.ds(at, 1), :] * mine

    def all_hot(p, carry):
        pick_hot(p)
        return carry
    lax.fori_loop(0, peers, all_hot, 0)

    def send_hot(px, py, p):
        pltpu.make_async_remote_copy(
            src_ref=hot_stage.at[p], dst_ref=hot_in.at[me], send_sem=hot_send, recv_sem=hot_recv,
            device_id=(px, py), device_id_type=MESH).start()
    others(send_hot)
    hot_in[me] = hot_stage[me]

    some = pl.ds(0, peers - 1)
    pltpu.make_async_copy(idx_in.at[some], idx_in.at[some], idx_recv).wait()
    to_smem = pltpu.make_async_copy(idx_in, idx_s, idx_local)
    to_smem.start()
    to_smem.wait()

    def pick(p):
        for t in range(tcount):
            for c in range(cap):
                k = t * cap + c
                stage[p, k:k + 1, :] = tab[t, pl.ds(idx_s[p, 0, k], 1), :]

    def send_cold(px, py, p):
        pltpu.make_async_remote_copy(
            src_ref=stage.at[p], dst_ref=recv.at[me], send_sem=cold_send, recv_sem=cold_recv,
            device_id=(px, py), device_id_type=MESH).start()

    def cold_step(i, carry):
        @pl.when(i < peers)
        def _():
            pick(peer(i)[2])

        @pl.when(jnp.logical_and(i > 0, i - 1 != self_at))
        def _():
            send_cold(*peer(i - 1))
        return carry
    lax.fori_loop(0, peers + 1, cold_step, 0)
    recv[me] = stage[me]

    pltpu.make_async_copy(hot_in.at[some], hot_in.at[some], hot_recv).wait()
    mine_at = pl.ds(pl.multiple_of(me * share, share), share)
    hot_tab[mine_at, :] = jnp.sum(hot_in[...], axis=0)

    slots = peers * cap
    col = lax.broadcasted_iota(jnp.int32, (cap, slots), 1)
    spread = (lax.rem(col, cap) == lax.broadcasted_iota(jnp.int32, (cap, slots), 0)).astype(jnp.float32)
    owner = lax.broadcasted_iota(jnp.int32, (peers, slots), 1) // cap
    mask = owner == lax.broadcasted_iota(jnp.int32, (peers, slots), 0)
    samples = lax.broadcasted_iota(jnp.int32, (batch, slots), 0).astype(jnp.float32)
    for t in range(tcount):
        wide = jnp.dot(bags_ref[0, t].astype(jnp.float32), spread,
                       precision=lax.Precision.HIGHEST, preferred_element_type=jnp.float32)
        flat = jnp.sum(jnp.where(mask, wide, 0.0), axis=0, keepdims=True)
        onehot[t] = (flat == samples).astype(jnp.bfloat16)

    def send_gat(px, py, p):
        pltpu.make_async_remote_copy(
            src_ref=hot_tab.at[mine_at], dst_ref=hot_tab.at[mine_at], send_sem=gat_send,
            recv_sem=gat_recv, device_id=(px, py), device_id_type=MESH).start()
    others(send_gat)

    ids_count = hot_ids_ref.shape[1] // tcount
    entry = lax.broadcasted_iota(jnp.int32, (batch, hot), 1)
    ids = hot_ids_ref[...]
    for t in range(tcount):
        total = jnp.zeros((batch, hot), jnp.float32)
        for k in range(ids_count):
            c = t * ids_count + k
            total += (ids[:, c:c + 1] == entry).astype(jnp.float32)
        counts[t] = total.astype(jnp.bfloat16)

    pltpu.make_async_copy(recv.at[some], recv.at[some], cold_recv).wait()
    for t in range(tcount):
        got = recv[:, t * cap:(t + 1) * cap, :].reshape(slots, width)
        out_ref[:, t * width:(t + 1) * width] = pool(onehot[t], got)
    rest = pl.ds(0, (peers - 1) * share)
    pltpu.make_async_copy(hot_tab.at[rest], hot_tab.at[rest], gat_recv).wait()
    for t in range(tcount):
        out_ref[:, t * width:(t + 1) * width] += pool(counts[t], hot_tab[t * hot:(t + 1) * hot, :])

    pltpu.make_async_copy(idx_out.at[some], idx_out.at[some], idx_send).wait()
    pltpu.make_async_copy(hot_stage.at[some], hot_stage.at[some], hot_send).wait()
    pltpu.make_async_copy(stage.at[some], stage.at[some], cold_send).wait()
    pltpu.make_async_copy(hot_tab.at[rest], hot_tab.at[rest], gat_send).wait()


def solution(mesh):
    nx, ny = mesh.shape["gx"], mesh.shape["gy"]
    peers = nx * ny

    def body(tables, cold_rows, cold_bags, hot_rows, hot_ids):
        tcount, rows_dev, width = tables.shape
        cap = cold_rows.shape[3]
        batch = hot_ids.shape[0]
        hot = hot_rows.shape[1]
        share = tcount * hot // peers
        assert share * peers == tcount * hot and hot % share == 0
        lanes = -(-tcount * cap // 128) * 128
        vmem = pl.BlockSpec(memory_space=pltpu.VMEM)
        out = pl.pallas_call(
            functools.partial(kernel, nx, ny),
            out_shape=jax.ShapeDtypeStruct((batch, tcount * width), jnp.float32),
            in_specs=[
                pl.BlockSpec(memory_space=pl.ANY), vmem, vmem,
                pl.BlockSpec(memory_space=pltpu.SMEM), vmem,
            ],
            out_specs=vmem,
            scratch_shapes=[
                pltpu.VMEM((tcount, rows_dev, width), jnp.float32),
                pltpu.VMEM((peers, 1, lanes), jnp.int32),
                pltpu.VMEM((peers, 1, lanes), jnp.int32),
                pltpu.SMEM((peers, 1, lanes), jnp.int32),
                pltpu.VMEM((peers, tcount * cap, width), jnp.float32),
                pltpu.VMEM((peers, tcount * cap, width), jnp.float32),
                pltpu.VMEM((peers, share, width), jnp.float32),
                pltpu.VMEM((peers, share, width), jnp.float32),
                pltpu.VMEM((tcount * hot, width), jnp.float32),
                pltpu.VMEM((tcount, batch, peers * cap), jnp.bfloat16),
                pltpu.VMEM((tcount, batch, hot), jnp.bfloat16),
                pltpu.SemaphoreType.DMA((tcount, CHUNKS)),
            ] + [pltpu.SemaphoreType.DMA] * 9,
            compiler_params=pltpu.CompilerParams(
                collective_id=0, has_side_effects=True, vmem_limit_bytes=48 * 1024 * 1024),
        )(tables, cold_rows, cold_bags, hot_rows, hot_ids.reshape(batch, -1))
        return out.reshape(batch, tcount, width)

    return jax.shard_map(
        body,
        mesh=mesh,
        in_specs=(
            P(None, ("gx", "gy"), None),
            P(("gx", "gy"), None, None, None),
            P(("gx", "gy"), None, None, None),
            P(),
            P(("gx", "gy"), None, None),
        ),
        out_specs=P(("gx", "gy"), None, None),
        check_vma=False,
    )
```

time: 204 us -> 39.9 us (0.20)
  waiting for transfers between devices: 139 us -> 0 us
  Pallas kernels: 0 us -> 35.7 us
  matrix products: 32.8 us -> 0 us
  between operations: 13.5 us -> 0.02 us
  starting transfers between devices: 12.7 us -> 0 us
    psum x1 -> x0, waiting for transfers between devices: 123 us -> none  [body(): hot_table = lax.psum(picked, ('gx', 'gy'))]
    pallas_call x0 -> x1, Pallas kernels: none -> 35.7 us  [body(): pl.pallas_call(functools.partial(kernel, nx, ny), out_shape=jax.ShapeDtyp...]
    dot_general x4 -> x0, matrix products: 32.8 us -> none  [the longest x2 29.7 us: one_block(): jnp.dot(selector, table, precision=lax.Precision.HIGHEST, preferred_eleme...]
    all_to_all x3 -> x0, waiting for transfers between devices: 15.7 us -> none  [the longest x1 7.25 us: body(): lax.all_to_all(my_bags, ('gx', 'gy'), split_axis=1, concat_axis=1, tiled=...]
    all_to_all x3 -> x0, starting transfers between devices: 12.5 us -> none  [the longest x1 7.33 us: body(): lax.all_to_all(my_rows, ('gx', 'gy'), split_axis=1, concat_axis=1, tiled=...]
  transfers between devices with their start and end apart: 4 -> 0, of which waited for: 4 -> 0; matrix products, arithmetic and copies ran while one was open for 8% -> 0% of each run, Pallas kernels for 0% -> 0%
where the time goes in v1:
time: 39.9 us; the launch traced here: 39.5 us
  Pallas kernels  35.7 us (89%)
  local copies, waits for them, and re-layouts  3.78 us (9%)
    pallas_call x1, Pallas kernels, body(): pl.pallas_call(functools.partial(kernel, nx, ny), out_shape=jax.ShapeDtyp...  35.7 us
    unnamed x4, local copies, waits for them, and re-layouts  2.26 us

profile of v1, /device:TPU:0, one launch (start us, length us, event | category | flops | bytes accessed | tf_op | source)
XLA Modules:
  0.0 39.5 jit_solution(10381102802032222062)
XLA Ops:
  0.0 0.8 %copy.9.rows_ref = s32[1,2,32,16]{3,2,1,0:T(8,128)S(1)} copy(s32[1,2,32,16]{2,3,1,0:T(8,128)} %param.6) | data formatting | bytes 8192 | tf_op args[1]
  0.8 0.8 %copy.10.bags_ref = s32[1,2,32,16]{3,2,1,0:T(8,128)S(1)} copy(s32[1,2,32,16]{2,3,1,0:T(8,128)} %param.7) | data formatting | bytes 8192 | tf_op args[2]
  1.6 0.8 %copy.11.hot_ids_ref = s32[128,16]{1,0:T(8,128)S(1)} copy(s32[128,16]{0,1:T(8,128)} %bitcast.1) | data formatting | bytes 16384 | tf_op jit(solution)/shard_map/reshape | solution.py:219
  2.4 0.0 copy-start
  2.4 0.7 %copy-done = s32[2,256]{1,0:T(2,128)S(1)} copy-done((s32[2,256]{1,0:T(2,128)S(1)}, s32[2,256]{1,0:T(2,128)}, u32[]{:S(2)}) %copy-start) | copy-done | bytes 2072
  3.1 35.7 %shard_map.55 = f32[128,256]{1,0:T(8,128)S(1)} custom-call(f32[2,8192,128]{2,1,0:T(8,128)} %tables_ref.1, s32[1,2,32,16]{3,2,1,0:T(8,128)S(1)} %copy.9.rows_ref, s32[1,2,32,16]{3,2,1,0:T(8,128)S(1)} %copy.10.bags_ref, s32[2,256]{1,0:T(2,128)S(1)} %copy-done, s32[128,16]{1,0:T(8,128)S(1)} %copy.11.hot_ids_ref), custom_call_target="tpu_custom_call" | custom-call | tf_op jit(solution)/shard_map/pallas_call | solution.py:195
  38.8 0.7 %reshape.7 = f32[128,2,128]{2,1,0:T(2,128)} reshape(f32[128,256]{1,0:T(8,128)S(1)} %shard_map.55) | data formatting | bytes 262144 | tf_op jit(solution)/shard_map/reshape | solution.py:220
Async XLA Ops:
  2.4 0.7 %copy-start = (s32[2,256]{1,0:T(2,128)S(1)}, s32[2,256]{1,0:T(2,128)}, u32[]{:S(2)}) copy-start(s32[2,256]{1,0:T(2,128)} %hot_rows_ref.1) | copy-start | bytes 6148

commit v2 on v1

v2 whole, which is shorter than its diff:
```python
import functools
import math

import jax
import jax.numpy as jnp
from jax import lax
from jax.experimental import pallas as pl
from jax.experimental.pallas import tpu as pltpu
from jax.sharding import PartitionSpec as P

MESH = pl.DeviceIdType.MESH
CHUNKS = 4
EARLY = 0.0


def ORDER(i, nx, ny):
    return i // ny, lax.rem(i, ny)


def split2(x):
    hi = x.astype(jnp.bfloat16)
    return hi, (x - hi.astype(jnp.float32)).astype(jnp.bfloat16)


def pool(weights, values):
    hi, lo = split2(values)
    return jnp.dot(weights, hi, preferred_element_type=jnp.float32) + jnp.dot(
        weights, lo, preferred_element_type=jnp.float32
    )


def kernel(nx, ny, tables_ref, rows_hbm, bags_hbm, hot_rows_hbm, hot_ids_hbm, out_ref,
           tab, rows_ref, bags_ref, hot_rows_ref, hot_ids_ref,
           idx_out, idx_s, stage, recv, hot_stage, hot_in, hot_part, hot_z, hot_tab,
           onehot, counts, tab_sem, in_sem, idx_send, idx_recv, idx_local, cold_send, cold_recv,
           hot_send, hot_recv, z_send, z_recv, gat_send, gat_recv):
    peers = nx * ny
    half = nx // 2
    tcount, rows_dev, width = tab.shape
    cap = rows_ref.shape[1]
    hot = hot_rows_ref.shape[1]
    chunk = hot_tab.shape[0] // ny
    batch = out_ref.shape[0]
    gx, gy = lax.axis_index("gx"), lax.axis_index("gy")
    me = gx * ny + gy

    def peer(i):
        m, j = ORDER(i, nx, ny)
        px = lax.rem(gx // half + 1 + m // half, 2) * half + lax.rem(gx + m, half)
        py = lax.rem(gy + j, ny)
        return px, py, px * ny + py

    def others(fn):
        def step(i, carry):
            px, py, p = peer(i)

            @pl.when(p != me)
            def _():
                fn(px, py, p)
            return carry
        lax.fori_loop(0, peers, step, 0)

    def plane_others(fn):
        def step(j, carry):
            fn(lax.rem(gy + j, ny))
            return carry
        lax.fori_loop(1, ny, step, 0)

    small = []
    for n, (src, dst) in enumerate(((rows_hbm, rows_ref), (hot_rows_hbm, hot_rows_ref),
                                    (bags_hbm, bags_ref), (hot_ids_hbm, hot_ids_ref))):
        load = pltpu.make_async_copy(src, dst, in_sem.at[n])
        load.start()
        small.append(load)

    piece = rows_dev // CHUNKS
    loads = []
    for t in range(tcount):
        for c in range(CHUNKS):
            part = pl.ds(c * piece, piece)
            load = pltpu.make_async_copy(tables_ref.at[t, part], tab.at[t, part], tab_sem.at[t, c])
            load.start()
            loads.append(load)

    barrier = pltpu.get_barrier_semaphore()
    others(lambda px, py, p: pl.semaphore_signal(
        barrier, inc=1, device_id=(px, py), device_id_type=MESH))

    small[0].wait()
    lines = rows_ref[...].reshape(tcount * cap, peers).T
    for p in range(peers):
        idx_out[p, :, 0:tcount * cap] = lines[p:p + 1, :]
    pl.semaphore_wait(barrier, peers - 1)

    own_idx = pltpu.make_async_copy(idx_out.at[me], idx_s.at[me], idx_local)
    own_idx.start()

    def send_idx(px, py, p):
        pltpu.make_async_remote_copy(
            src_ref=idx_out.at[p], dst_ref=idx_s.at[me], send_sem=idx_send, recv_sem=idx_recv,
            device_id=(px, py), device_id_type=MESH).start()
    others(send_idx)

    small[1].wait()
    for load in loads:
        load.wait()

    base = me * rows_dev
    group = math.gcd(chunk, 16)

    def pick_hot(y):
        def rows_of(g, carry):
            start = y * chunk + g * group
            t = start // hot
            first = start - t * hot
            for j in range(group):
                local = hot_rows_ref[t, first + j] - base
                mine = jnp.logical_and(local >= 0, local < rows_dev).astype(jnp.float32)
                at = jnp.clip(local, 0, rows_dev - 1)
                hot_stage[y, pl.ds(g * group + j, 1), :] = tab[t, pl.ds(at, 1), :] * mine
            return carry
        lax.fori_loop(0, chunk // group, rows_of, 0)

    def send_hot(y):
        pltpu.make_async_remote_copy(
            src_ref=hot_stage.at[y], dst_ref=hot_in.at[gy], send_sem=hot_send, recv_sem=hot_recv,
            device_id=(gx, y), device_id_type=MESH).start()

    def hot_step(j, carry):
        pick_hot(lax.rem(gy + j, ny))

        @pl.when(j > 1)
        def _():
            send_hot(lax.rem(gy + j - 1, ny))
        return carry
    lax.fori_loop(1, ny + 1, hot_step, 0)
    hot_in[gy] = hot_stage[gy]

    some = pl.ds(0, peers - 1)
    pltpu.make_async_copy(idx_s.at[some], idx_s.at[some], idx_recv).wait()
    own_idx.wait()

    def pick(p):
        for t in range(tcount):
            for c in range(cap):
                k = t * cap + c
                stage[p, k:k + 1, :] = tab[t, pl.ds(idx_s[p, 0, k], 1), :]

    def send_cold(i):
        px, py, p = peer(i)

        @pl.when(p != me)
        def _():
            pltpu.make_async_remote_copy(
                src_ref=stage.at[p], dst_ref=recv.at[me], send_sem=cold_send, recv_sem=cold_recv,
                device_id=(px, py), device_id_type=MESH).start()

    def cold_steps(first, last):
        def step(i, carry):
            pick(peer(i)[2])

            @pl.when(i > 0)
            def _():
                send_cold(i - 1)
            return carry
        lax.fori_loop(first, last, step, 0)

    early = int(peers * EARLY)
    cold_steps(0, early)

    planes = pl.ds(0, ny - 1)
    pltpu.make_async_copy(hot_in.at[planes], hot_in.at[planes], hot_recv).wait()
    hot_part[...] = jnp.sum(hot_in[...], axis=0)
    hot_z[gx] = hot_part[...]
    cold_steps(early, early + 1)

    def send_z(k, carry):
        pltpu.make_async_remote_copy(
            src_ref=hot_part, dst_ref=hot_z.at[gx], send_sem=z_send, recv_sem=z_recv,
            device_id=(lax.rem(gx + k, nx), gy), device_id_type=MESH).start()
        return carry
    lax.fori_loop(1, nx, send_z, 0)
    cold_steps(early + 1, peers)
    recv[me] = stage[me]
    small[2].wait()
    small[3].wait()
    send_cold(peers - 1)

    slots = peers * cap
    owner = lax.broadcasted_iota(jnp.int32, (peers, slots), 1) // cap
    spread = (owner == lax.broadcasted_iota(jnp.int32, (peers, slots), 0)).astype(jnp.float32)
    place = lax.rem(lax.broadcasted_iota(jnp.int32, (cap, slots), 1), cap)
    mask = place == lax.broadcasted_iota(jnp.int32, (cap, slots), 0)
    samples = lax.broadcasted_iota(jnp.int32, (batch, slots), 0).astype(jnp.float32)

    def cold_weights(t):
        wide = jnp.dot(bags_ref[t].astype(jnp.float32), spread,
                       precision=lax.Precision.HIGHEST, preferred_element_type=jnp.float32)
        flat = jnp.sum(jnp.where(mask, wide, 0.0), axis=0, keepdims=True)
        onehot[t] = (flat == samples).astype(jnp.bfloat16)

    cold_weights(0)

    zs = pl.ds(0, nx - 1)
    pltpu.make_async_copy(hot_z.at[zs], hot_z.at[zs], z_recv).wait()
    mine_at = pl.ds(pl.multiple_of(gy * chunk, chunk), chunk)
    hot_tab[mine_at, :] = jnp.sum(hot_z[...], axis=0)
    for t in range(1, tcount):
        cold_weights(t)

    def send_gat(y):
        pltpu.make_async_remote_copy(
            src_ref=hot_tab.at[mine_at], dst_ref=hot_tab.at[mine_at], send_sem=gat_send,
            recv_sem=gat_recv, device_id=(gx, y), device_id_type=MESH).start()
    plane_others(send_gat)

    entry = lax.broadcasted_iota(jnp.int32, (hot, batch), 0)
    for t in range(tcount):
        total = jnp.zeros((hot, batch), jnp.float32)
        for k in range(hot_ids_ref.shape[1]):
            total += (hot_ids_ref[t, k:k + 1, :] == entry).astype(jnp.float32)
        counts[t] = total.T.astype(jnp.bfloat16)

    rest = pl.ds(0, (ny - 1) * chunk)

    def pool_cold():
        pltpu.make_async_copy(recv.at[some], recv.at[some], cold_recv).wait()
        return [pool(onehot[t], recv[:, t * cap:(t + 1) * cap, :].reshape(slots, width))
                for t in range(tcount)]

    def pool_hot():
        pltpu.make_async_copy(hot_tab.at[rest], hot_tab.at[rest], gat_recv).wait()
        return [pool(counts[t], hot_tab[t * hot:(t + 1) * hot, :]) for t in range(tcount)]

    for t, part in enumerate(pool_cold()):
        out_ref[:, t * width:(t + 1) * width] = part
    for t, part in enumerate(pool_hot()):
        out_ref[:, t * width:(t + 1) * width] += part

    pltpu.make_async_copy(idx_out.at[some], idx_out.at[some], idx_send).wait()
    pltpu.make_async_copy(hot_stage.at[planes], hot_stage.at[planes], hot_send).wait()
    pltpu.make_async_copy(stage.at[some], stage.at[some], cold_send).wait()
    pltpu.make_async_copy(hot_z.at[zs], hot_z.at[zs], z_send).wait()
    pltpu.make_async_copy(hot_tab.at[rest], hot_tab.at[rest], gat_send).wait()


def solution(mesh):
    nx, ny = mesh.shape["gx"], mesh.shape["gy"]
    peers = nx * ny

    def body(tables, cold_rows, cold_bags, hot_rows, hot_ids):
        tcount, rows_dev, width = tables.shape
        cap = cold_rows.shape[3]
        batch = hot_ids.shape[0]
        hot = hot_rows.shape[1]
        chunk = tcount * hot // ny
        assert nx % 2 == 0 and chunk * ny == tcount * hot and hot % math.gcd(chunk, 16) == 0
        lanes = -(-tcount * cap // 128) * 128
        rows_t = jnp.transpose(cold_rows[0], (0, 2, 1))
        bags_t = jnp.transpose(cold_bags[0], (0, 2, 1))
        ids_t = jnp.transpose(hot_ids, (1, 2, 0))
        hbm = pl.BlockSpec(memory_space=pltpu.HBM)
        out = pl.pallas_call(
            functools.partial(kernel, nx, ny),
            out_shape=jax.ShapeDtypeStruct((batch, tcount * width), jnp.float32),
            in_specs=[hbm] * 5,
            out_specs=pl.BlockSpec(memory_space=pltpu.VMEM),
            scratch_shapes=[
                pltpu.VMEM((tcount, rows_dev, width), jnp.float32),
                pltpu.VMEM(rows_t.shape, jnp.int32),
                pltpu.VMEM(bags_t.shape, jnp.int32),
                pltpu.SMEM(hot_rows.shape, jnp.int32),
                pltpu.VMEM(ids_t.shape, jnp.int32),
                pltpu.VMEM((peers, 1, lanes), jnp.int32),
                pltpu.SMEM((peers, 1, lanes), jnp.int32),
                pltpu.VMEM((peers, tcount * cap, width), jnp.float32),
                pltpu.VMEM((peers, tcount * cap, width), jnp.float32),
                pltpu.VMEM((ny, chunk, width), jnp.float32),
                pltpu.VMEM((ny, chunk, width), jnp.float32),
                pltpu.VMEM((chunk, width), jnp.float32),
                pltpu.VMEM((nx, chunk, width), jnp.float32),
                pltpu.VMEM((tcount * hot, width), jnp.float32),
                pltpu.VMEM((tcount, batch, peers * cap), jnp.bfloat16),
                pltpu.VMEM((tcount, batch, hot), jnp.bfloat16),
                pltpu.SemaphoreType.DMA((tcount, CHUNKS)),
                pltpu.SemaphoreType.DMA((4,)),
            ] + [pltpu.SemaphoreType.DMA] * 11,
            compiler_params=pltpu.CompilerParams(
                collective_id=0, has_side_effects=True, vmem_limit_bytes=67043328),
        )(tables, rows_t, bags_t, hot_rows, ids_t)
        return out.reshape(batch, tcount, width)

    return jax.shard_map(
        body,
        mesh=mesh,
        in_specs=(
            P(None, ("gx", "gy"), None),
            P(("gx", "gy"), None, None, None),
            P(("gx", "gy"), None, None, None),
            P(),
            P(("gx", "gy"), None, None),
        ),
        out_specs=P(("gx", "gy"), None, None),
        check_vma=False,
    )
```

time: 39.9 us -> 31.2 us (0.78)
  Pallas kernels: 35.7 us -> 29.1 us
  local copies, waits for them, and re-layouts: 3.78 us -> 1.62 us
    pallas_call x1, Pallas kernels: 35.7 us -> 29.1 us  [body(): pl.pallas_call(functools.partial(kernel, nx, ny), out_shape=jax.ShapeDtyp...]
    unnamed x4 -> x0, local copies, waits for them, and re-layouts: 2.26 us -> none
    reshape x1, local copies, waits for them, and re-layouts: 0.72 us -> 1.62 us  [body(): return out.reshape(batch, tcount, width)]
    reshape x1 -> x0, local copies, waits for them, and re-layouts: 0.8 us -> none  [body(): hot_ids.reshape(batch, -1)]
where the time goes in v2:
time: 31.2 us; the launch traced here: 30.7 us
  Pallas kernels  29.1 us (93%)
  local copies, waits for them, and re-layouts  1.62 us (5%)
    pallas_call x1, Pallas kernels, body(): pl.pallas_call(functools.partial(kernel, nx, ny), out_shape=jax.ShapeDtyp...  29.1 us
    reshape x1, local copies, waits for them, and re-layouts, body(): return out.reshape(batch, tcount, width)  1.62 us

profile of v2, /device:TPU:0, one launch (start us, length us, event | category | flops | bytes accessed | tf_op | source)
XLA Modules:
  0.0 30.7 jit_solution(10590711067178134807)
XLA Ops:
  0.0 29.1 %shard_map.55 = f32[128,256]{1,0:T(8,128)} custom-call(f32[2,8192,128]{2,1,0:T(8,128)} %tables_ref.1, s32[2,16,32]{2,1,0:T(8,128)} %bitcast.7, s32[2,16,32]{2,1,0:T(8,128)} %bitcast.8, s32[2,256]{1,0:T(2,128)} %hot_rows_hbm.1, s32[2,8,128]{2,1,0:T(8,128)} %bitcast.9), custom_call_target="tpu_custom_call" | custom-call | tf_op jit(solution)/shard_map/pallas_call | solution.py:263
  29.1 1.6 %reshape.3 = f32[128,2,128]{2,1,0:T(2,128)} reshape(f32[128,256]{1,0:T(8,128)} %shard_map.55) | data formatting | bytes 262144 | tf_op jit(solution)/shard_map/reshape | solution.py:291
